TPU v7x, 32 devices: a 4x4x1 block of a 4x4x8 slice. The times are simulated.
32 devices in a mesh: problem: 1 (over z), samp: 4 (over y), feat: 8 (over x, core).
Axes of the slice: x: 4, y: 4, z: 1, core: 2. Of those that a mesh axis runs over, the one named last changes fastest.
The devices are a block of a 4x4x8 slice.
Arguments:
- design: bfloat16 [512, 1048576], P(('problem', 'samp'), 'feat')
- targets: float32 [512, 32], P(('problem', 'samp'))
- coef_init: float32 [1048576, 32], P(('problem', 'feat'))
- step_sizes: float32 [1048576], P(('problem', 'feat'))
- ridge_weights: float32 [32], P('problem')
Outputs:
- output 1: float32 [1048576, 32], P(('problem', 'feat'))
- output 2: float32 [512, 32], P(('problem', 'samp'))
All inputs are finite; a program needn't handle non-finite values.
Results may differ from a plain program's by a relative error of at most 0.00635085.
Values are sent between devices in bfloat16 or wider.
A program may use at most 768 MiB of HBM per device.

v0:
```python
import jax
import jax.numpy as jnp
from jax import lax
from jax.sharding import PartitionSpec as P

SWEEPS = 4
STEP_WEIGHT = 0.5


def solution(mesh):
    samp_size = mesh.shape["samp"]
    design_spec = P(("problem", "samp"), "feat")
    rows_spec = P(("problem", "samp"), None)
    coef_spec = P(("problem", "feat"), None)
    step_spec = P(("problem", "feat"))
    ridge_spec = P("problem")

    def local_sweeps(design, targets, coef_init, step_sizes, ridge_weights):
        total_rows = design.shape[0] * samp_size
        step_col = step_sizes[:, None]
        ridge_row = ridge_weights[None, :]

        def block_product(weights):
            product = jnp.dot(design, weights.astype(jnp.bfloat16), preferred_element_type=jnp.float32)
            return product.astype(jnp.bfloat16).astype(jnp.float32)

        resid_cur = targets - lax.psum(block_product(coef_init), "feat")
        coef_cur = coef_init
        for sweep_index in range(SWEEPS):
            part_grad = lax.dot_general(design, resid_cur.astype(jnp.bfloat16), (((0,), (0,)), ((), ())), preferred_element_type=jnp.float32)
            gradient = lax.psum(part_grad, "samp") / total_rows
            step_delta = step_col * (gradient - ridge_row * coef_cur)
            coef_cur = coef_cur + STEP_WEIGHT * step_delta
            resid_cur = resid_cur - STEP_WEIGHT * lax.psum(block_product(step_delta), "feat")
        return coef_cur, resid_cur

    return jax.shard_map(local_sweeps, mesh=mesh, in_specs=(design_spec, rows_spec, coef_spec, step_spec, ridge_spec), out_specs=(coef_spec, rows_spec), check_vma=False)
```

profile of v0, /device:TPU:97, one launch (start us, length us, event | category | flops | bytes accessed | tf_op | source)
XLA Modules:
  0.0 1518.9 jit_solution(5451963765090688463)
XLA Ops:
  7.2 0.0 copy-start.2
  7.2 0.1 all-reduce.5.cloned.1.call-start
  7.3 21.0 %fusion.29 = f32[128,32]{0,1:T(8,128)S(1)} fusion(bf16[128,131072]{1,0:T(8,128)(2,1)} %param.5, f32[131072,32]{0,1:T(8,128)} %param.7), kind=kOutput, calls=%fused_computation.35 | convolution fusion | flops 1077944320 | bytes 50348032 | tf_op jit(solution)/shard_map/dot_general | solution.py:24
  28.3 24.0 %psum.63 = f32[128,32]{0,1:T(8,128)S(1)} all-reduce(f32[128,32]{0,1:T(8,128)S(1)} %fusion.29), channel_id=1, replica_groups=mesh['problem'=1,'samp'=4,'feat'=8] {'feat'}, use_global_device_ids=true, to_apply=%region_0.0 | all-reduce | flops 4096 | bytes 32768 | tf_op jit(solution)/shard_map/psum | solution.py:27
  52.3 0.0 copy-done.2
  52.3 19.3 %convolution_bitcast_fusion.3 = f32[131072,32]{0,1:T(8,128)} fusion(bf16[128,131072]{1,0:T(8,128)(2,1)} %param.5, f32[128,32]{0,1:T(8,128)S(1)} %sub.27), kind=kOutput, calls=%fused_computation.3 | convolution fusion | flops 1073745920 | bytes 50348032 | tf_op jit(solution)/shard_map/dot_general | solution.py:30
  71.6 0.0 copy-start
  71.6 0.0 copy-start.1
  71.6 0.1 all-reduce.5.cloned.1.call-update
  71.7 0.1 all-reduce.7.cloned.1.call-start
  71.8 293.3 %all-reduce.5.cloned.1.call-done = f32[131072,32]{0,1:T(8,128)} async-done(((f32[131072,32]{0,1:T(8,128)}), f32[131072,32]{0,1:T(8,128)}) %all-reduce.5.cloned.1.call-update) | async-done | bytes 16777232 | tf_op jit(solution)/shard_map/psum | solution.py:31
  365.1 0.0 copy-done
  365.1 0.0 copy-done.1
  365.1 23.4 %fusion.38 = f32[128,32]{0,1:T(8,128)S(1)} fusion(bf16[128,131072]{1,0:T(8,128)(2,1)} %param.5, f32[131072,32]{0,1:T(8,128)} %param.7, f32[131072,32]{0,1:T(8,128)} %all-reduce.5.cloned.1.call-done, f32[32]{0:T(128)S(1)} %copy-done.1, f32[131072]{0:T(1024)S(1)} %copy-done), kind=kOutput, calls=%fused_computation.38 | convolution fusion | flops 1094721536 | bytes 67649664 | tf_op jit(solution)/shard_map/dot_general | solution.py:24
  388.5 22.7 %psum.65 = f32[128,32]{0,1:T(8,128)S(1)} all-reduce(f32[128,32]{0,1:T(8,128)S(1)} %fusion.38), channel_id=1, replica_groups=mesh['problem'=1,'samp'=4,'feat'=8] {'feat'}, use_global_device_ids=true, to_apply=%region_2.0 | all-reduce | flops 4096 | bytes 32768 | tf_op jit(solution)/shard_map/psum | solution.py:34
  411.2 19.3 %convolution_bitcast_fusion.2 = f32[131072,32]{0,1:T(8,128)} fusion(bf16[128,131072]{1,0:T(8,128)(2,1)} %param.5, f32[128,32]{0,1:T(8,128)S(1)} %sub.27, f32[128,32]{0,1:T(8,128)S(1)} %psum.65), kind=kOutput, calls=%fused_computation.2 | convolution fusion | flops 1073754112 | bytes 50364416 | tf_op jit(solution)/shard_map/dot_general | solution.py:30
  430.5 0.1 all-reduce.7.cloned.1.call-update
  430.6 0.1 all-reduce.9.cloned.1.call-start
  430.6 290.3 %all-reduce.7.cloned.1.call-done = f32[131072,32]{0,1:T(8,128)} async-done(((f32[131072,32]{0,1:T(8,128)}), f32[131072,32]{0,1:T(8,128)}) %all-reduce.7.cloned.1.call-update) | async-done | bytes 16777232 | tf_op jit(solution)/shard_map/psum | solution.py:31
  720.9 28.2 %fusion.47 = f32[128,32]{0,1:T(8,128)S(1)} fusion(bf16[128,131072]{1,0:T(8,128)(2,1)} %param.5, f32[131072,32]{0,1:T(8,128)} %all-reduce.7.cloned.1.call-done, f32[32]{0:T(128)S(1)} %copy-done.1, f32[131072]{0:T(1024)S(1)} %copy-done, f32[131072,32]{0,1:T(8,128)} %param.7, f32[131072,32]{0,1:T(8,128)} %all-reduce.5.cloned.1.call-done), kind=kOutput, calls=%fused_computation.41 | convolution fusion | flops 1119887360 | bytes 84426880 | tf_op jit(solution)/shard_map/dot_general | solution.py:24
  749.1 22.7 %psum.67 = f32[128,32]{0,1:T(8,128)S(1)} all-reduce(f32[128,32]{0,1:T(8,128)S(1)} %fusion.47), channel_id=1, replica_groups=mesh['problem'=1,'samp'=4,'feat'=8] {'feat'}, use_global_device_ids=true, to_apply=%region_4.0 | all-reduce | flops 4096 | bytes 32768 | tf_op jit(solution)/shard_map/psum | solution.py:34
  771.9 19.1 %convolution_bitcast_fusion.1 = f32[131072,32]{0,1:T(8,128)} fusion(bf16[128,131072]{1,0:T(8,128)(2,1)} %param.5, f32[128,32]{0,1:T(8,128)S(1)} %multiply_subtract_fusion.2), kind=kOutput, calls=%fused_computation.1 | convolution fusion | flops 1073745920 | bytes 50348032 | tf_op jit(solution)/shard_map/dot_general | solution.py:30
  791.0 0.1 all-reduce.9.cloned.1.call-update
  791.0 0.1 all-reduce.11.cloned.1.call-start
  791.1 23.8 %multiply_add_fusion.2 = f32[131072,32]{0,1:T(8,128)} fusion(f32[131072,32]{0,1:T(8,128)} %all-reduce.7.cloned.1.call-done, f32[32]{0:T(128)S(1)} %copy-done.1, f32[131072]{0:T(1024)S(1)} %copy-done, f32[131072,32]{0,1:T(8,128)} %param.7, f32[131072,32]{0,1:T(8,128)} %all-reduce.5.cloned.1.call-done), kind=kLoop, calls=%fused_computation.8 | loop fusion | flops 50331648 | bytes 67633280 | tf_op jit(solution)/shard_map/add | solution.py:33
  814.9 266.5 %all-reduce.9.cloned.1.call-done = f32[131072,32]{0,1:T(8,128)} async-done(((f32[131072,32]{0,1:T(8,128)}), f32[131072,32]{0,1:T(8,128)}) %all-reduce.9.cloned.1.call-update) | async-done | bytes 16777232 | tf_op jit(solution)/shard_map/psum | solution.py:31
  1081.4 23.4 %fusion.56 = f32[128,32]{0,1:T(8,128)S(1)} fusion(bf16[128,131072]{1,0:T(8,128)(2,1)} %param.5, f32[131072,32]{0,1:T(8,128)} %multiply_add_fusion.2, f32[131072,32]{0,1:T(8,128)} %all-reduce.9.cloned.1.call-done, f32[32]{0:T(128)S(1)} %copy-done.1, f32[131072]{0:T(1024)S(1)} %copy-done), kind=kOutput, calls=%fused_computation.44 | convolution fusion | flops 1094721536 | bytes 67649664 | tf_op jit(solution)/shard_map/dot_general | solution.py:24
  1104.8 22.7 %psum.69 = f32[128,32]{0,1:T(8,128)S(1)} all-reduce(f32[128,32]{0,1:T(8,128)S(1)} %fusion.56), channel_id=1, replica_groups=mesh['problem'=1,'samp'=4,'feat'=8] {'feat'}, use_global_device_ids=true, to_apply=%region_6.0 | all-reduce | flops 4096 | bytes 32768 | tf_op jit(solution)/shard_map/psum | solution.py:34
  1127.5 19.1 %convolution_bitcast_fusion = f32[131072,32]{0,1:T(8,128)} fusion(bf16[128,131072]{1,0:T(8,128)(2,1)} %param.5, f32[128,32]{0,1:T(8,128)S(1)} %multiply_subtract_fusion.2, f32[128,32]{0,1:T(8,128)S(1)} %psum.69), kind=kOutput, calls=%fused_computation | convolution fusion | flops 1073754112 | bytes 50364416 | tf_op jit(solution)/shard_map/dot_general | solution.py:30
  1146.6 0.1 all-reduce.11.cloned.1.call-update
  1146.6 290.4 %all-reduce.11.cloned.1.call-done = f32[131072,32]{0,1:T(8,128)} async-done(((f32[131072,32]{0,1:T(8,128)}), f32[131072,32]{0,1:T(8,128)}) %all-reduce.11.cloned.1.call-update) | async-done | bytes 16777232 | tf_op jit(solution)/shard_map/psum | solution.py:31
  1437.0 28.2 %fusion.65 = f32[128,32]{0,1:T(8,128)S(1)} fusion(bf16[128,131072]{1,0:T(8,128)(2,1)} %param.5, f32[131072,32]{0,1:T(8,128)} %all-reduce.11.cloned.1.call-done, f32[32]{0:T(128)S(1)} %copy-done.1, f32[131072]{0:T(1024)S(1)} %copy-done, f32[131072,32]{0,1:T(8,128)} %multiply_add_fusion.2, f32[131072,32]{0,1:T(8,128)} %all-reduce.9.cloned.1.call-done), kind=kOutput, calls=%fused_computation.47 | convolution fusion | flops 1119887360 | bytes 84426880 | tf_op jit(solution)/shard_map/dot_general | solution.py:24
  1465.2 22.7 %psum.71 = f32[128,32]{0,1:T(8,128)S(1)} all-reduce(f32[128,32]{0,1:T(8,128)S(1)} %fusion.65), channel_id=1, replica_groups=mesh['problem'=1,'samp'=4,'feat'=8] {'feat'}, use_global_device_ids=true, to_apply=%region_8.0 | all-reduce | flops 4096 | bytes 32768 | tf_op jit(solution)/shard_map/psum | solution.py:34
  1487.9 0.6 multiply_subtract_fusion
  1488.5 23.8 %multiply_add_fusion = f32[131072,32]{0,1:T(8,128)} fusion(f32[131072,32]{0,1:T(8,128)} %all-reduce.11.cloned.1.call-done, f32[32]{0:T(128)S(1)} %copy-done.1, f32[131072]{0:T(1024)S(1)} %copy-done, f32[131072,32]{0,1:T(8,128)} %multiply_add_fusion.2, f32[131072,32]{0,1:T(8,128)} %all-reduce.9.cloned.1.call-done), kind=kLoop, calls=%fused_computation.4 | loop fusion | flops 50331648 | bytes 67633280 | tf_op jit(solution)/shard_map/add | solution.py:33
  (2 shorter events, 0.0 us)
Async XLA Ops:
  7.2 45.2 %copy-start.2 = (f32[128,32]{0,1:T(8,128)S(1)}, f32[128,32]{0,1:T(8,128)}, u32[]{:S(2)}) copy-start(f32[128,32]{0,1:T(8,128)} %param.6) | copy-start | bytes 49156
  7.2 357.9 %all-reduce.5.cloned.1.call-start = ((), (), s32[]{:S(2)}) async-start(), calls=%async_computation | async-start | bytes 33554432 | tf_op jit(solution)/shard_map/psum | solution.py:31
  71.6 293.5 %copy-start = (f32[131072]{0:T(1024)S(1)}, f32[131072]{0:T(1024)}, u32[]{:S(2)}) copy-start(f32[131072]{0:T(1024)} %param.8) | copy-start | bytes 1572868
  71.6 293.5 %copy-start.1 = (f32[32]{0:T(128)S(1)}, f32[32]{0:T(128)}, u32[]{:S(2)}) copy-start(f32[32]{0:T(128)} %param.9) | copy-start | bytes 388
  71.7 649.2 %all-reduce.7.cloned.1.call-start = ((), (), s32[]{:S(2)}) async-start(), calls=%async_computation.1 | async-start | bytes 33554432 | tf_op jit(solution)/shard_map/psum | solution.py:31
  430.6 650.8 %all-reduce.9.cloned.1.call-start = ((), (), s32[]{:S(2)}) async-start(), calls=%async_computation.2 | async-start | bytes 33554432 | tf_op jit(solution)/shard_map/psum | solution.py:31
  791.0 646.0 %all-reduce.11.cloned.1.call-start = ((), (), s32[]{:S(2)}) async-start(), calls=%async_computation.3 | async-start | bytes 33554432 | tf_op jit(solution)/shard_map/psum | solution.py:31
Sparse Core Ops, SparseCore 0:
  71.8 293.2 all-reduce.4
  430.7 290.2 all-reduce.6
  791.1 290.2 all-reduce.8
  1146.7 290.2 all-reduce.10
where the time goes:
time: 1520 us
  waiting for transfers between devices  1140 us (75%)
  matrix products  201 us (13%)
  blocking collectives  115 us (8%)
  other arithmetic  48.3 us (3%)
    psum x4, waiting for transfers between devices, local_sweeps(): gradient = lax.psum(part_grad, 'samp') / total_rows  1140 us
    dot_general x5, matrix products, block_product(): jnp.dot(design, weights.astype(jnp.bfloat16), preferred_element_type=jnp....  124 us
    psum x4, blocking collectives, local_sweeps(): lax.psum(block_product(step_delta), 'feat')  90.9 us
    dot_general x4, matrix products, local_sweeps(): lax.dot_general(design, resid_cur.astype(jnp.bfloat16), (((0,), (0,)), ((...  76.8 us
    add x2, other arithmetic, local_sweeps(): coef_cur = coef_cur + STEP_WEIGHT * step_delta  47.7 us
  transfers between devices with their start and end apart: 4, of which 4 were waited for; matrix products, arithmetic and copies ran while one was open for 2% of the time, Pallas kernels for 0%

commit v1 on v0

v1 whole, which is shorter than its diff:
```python
import functools

import jax
import jax.numpy as jnp
from jax import lax
from jax.experimental import pallas as pl
from jax.experimental.pallas import tpu as pltpu
from jax.sharding import PartitionSpec as P

SWEEPS = 4
STEP_WEIGHT = 0.5
CHUNK = 1024
AHEAD = 6
STREAM = 4096
STREAM_BUFS = 4
GATHER_FIRST = 8
GATHER_AHEAD = 16
MESH = pl.DeviceIdType.MESH


def sweeps_kernel(
    ns, nf, total_rows,
    x_hbm, y_ref, w0_hbm, eta_hbm, lam_ref,
    wout_hbm, rout_ref,
    xs, relay, ws, eta, acc, sx, sw, p1s, p1, p2, rb,
    x_sem, xsend_sem, relay_sem, w_sem, eta_sem, sx_sem, sw_sem,
    p1_sem, p1s_sem, p2_sem, p2s_sem, p3_sem, p3s_sem,
    gd_sem, gf_sem, gs_sem,
):
    nch, rows_all, cc = xs.shape
    rows = rows_all // ns
    half = rows // 2
    targets = y_ref.shape[0]
    thalf = targets // 2
    quarter = nch * cc
    nstream = x_hbm.shape[1] // STREAM
    s = lax.axis_index("samp")
    f = lax.axis_index("feat")
    right, left, opp = lax.rem(s + 1, ns), lax.rem(s + ns - 1, ns), lax.rem(s + 2, ns)
    samp_peers = [lax.rem(s + k, ns) for k in range(1, ns)]
    feat_peers = [lax.rem(f + k, nf) for k in range(1, nf)]

    def remote(src, dst, send_sem, recv_sem, **where):
        return pltpu.make_async_remote_copy(
            src_ref=src, dst_ref=dst, send_sem=send_sem, recv_sem=recv_sem,
            device_id=where, device_id_type=MESH)

    def cols(owner, c):
        return pl.ds(pl.multiple_of(owner * quarter + c * cc, cc), cc)

    def wait_bytes(ref, sem):
        pltpu.make_async_copy(ref, ref, sem).wait()

    barrier = pltpu.get_barrier_semaphore()
    for peer in samp_peers:
        pl.semaphore_signal(barrier, inc=1, device_id={"samp": peer}, device_id_type=MESH)
    for peer in feat_peers:
        pl.semaphore_signal(barrier, inc=1, device_id={"feat": peer}, device_id_type=MESH)
    pl.semaphore_wait(barrier, ns - 1 + nf - 1)

    def issue_first(c):
        for part, peer in ((0, right), (1, left)):
            remote(x_hbm.at[pl.ds(part * half, half), cols(opp, c)], relay.at[c, part],
                   xsend_sem.at[c], relay_sem.at[c], samp=peer).start()

    def issue_direct(c):
        mine = pl.ds(pl.multiple_of(s * rows, rows), rows)
        for peer in (right, left):
            remote(x_hbm.at[:, cols(peer, c)], xs.at[c, mine, :],
                   xsend_sem.at[c], x_sem.at[c], samp=peer).start()
        pltpu.make_async_copy(x_hbm.at[:, cols(s, c)], xs.at[c, mine, :], x_sem.at[c]).start()
        pltpu.make_async_copy(w0_hbm.at[:, cols(s, c)], ws.at[c], w_sem.at[c]).start()

    def forward(c):
        wait_bytes(relay.at[c], relay_sem.at[c])
        remote(relay.at[c, 0], xs.at[c, pl.ds(pl.multiple_of(left * rows, rows), half), :],
               xsend_sem.at[c], x_sem.at[c], samp=right).start()
        remote(relay.at[c, 1], xs.at[c, pl.ds(pl.multiple_of(right * rows + half, half), half), :],
               xsend_sem.at[c], x_sem.at[c], samp=left).start()

    def stream_copies(i):
        slot = lax.rem(i, STREAM_BUFS)
        span = pl.ds(pl.multiple_of(i * STREAM, STREAM), STREAM)
        return (pltpu.make_async_copy(x_hbm.at[:, span], sx.at[slot], sx_sem.at[slot]),
                pltpu.make_async_copy(w0_hbm.at[:, span], sw.at[slot], sw_sem.at[slot]))

    issue_first(0)
    for i in range(STREAM_BUFS - 1):
        for copy in stream_copies(i):
            copy.start()

    def issue_step(c, carry):
        issue_first(c + 1)
        issue_direct(c)
        return carry

    lax.fori_loop(0, AHEAD, issue_step, 0)
    eta_copy = pltpu.make_async_copy(
        eta_hbm.at[:, pl.ds(pl.multiple_of(s * quarter, quarter), quarter)], eta, eta_sem)
    eta_copy.start()

    contract_last = (((1,), (1,)), ((), ()))

    def first_product(i, total):
        @pl.when(i + STREAM_BUFS - 1 < nstream)
        def _():
            for copy in stream_copies(i + STREAM_BUFS - 1):
                copy.start()

        for copy in stream_copies(i):
            copy.wait()
        slot = lax.rem(i, STREAM_BUFS)
        return total + lax.dot_general(
            sw[slot].astype(jnp.bfloat16), sx[slot], contract_last, preferred_element_type=jnp.float32)

    block_rows = lax.fori_loop(0, nstream, first_product, jnp.zeros((targets, rows), jnp.float32))

    def sum_blocks(r, block_rows):
        p2[r, f] = block_rows.astype(jnp.bfloat16)
        copies = [remote(p2.at[r, f], p2.at[r, f], p2s_sem.at[r], p2_sem.at[r], feat=peer) for peer in feat_peers]
        for copy in copies:
            copy.start()
        wait_bytes(p2.at[r, pl.ds(0, nf - 1)], p2_sem.at[r])
        wait_bytes(p2.at[r, pl.ds(0, nf - 1)], p2s_sem.at[r])
        total = p2[r, 0].astype(jnp.float32)
        for j in range(1, nf):
            total = total + p2[r, j].astype(jnp.float32)
        return total

    def share_resid(r, resid):
        rb[r, s] = resid.astype(jnp.bfloat16)
        for peer in samp_peers:
            remote(rb.at[r, s], rb.at[r, s], p3s_sem.at[r], p3_sem.at[r], samp=peer).start()
        wait_bytes(rb.at[r, pl.ds(0, ns - 1)], p3_sem.at[r])
        wait_bytes(rb.at[r, pl.ds(0, ns - 1)], p3s_sem.at[r])
        return jnp.concatenate([rb[r, q] for q in range(ns)], axis=1)

    def scatter_start(r):
        for q in range(ns):
            p1s[r - 1, q] = acc[:, q * rows:(q + 1) * rows]
        for peer in samp_peers:
            remote(p1s.at[r - 1, peer], p1.at[r - 1, s], p1s_sem.at[r - 1], p1_sem.at[r - 1], samp=peer).start()
        p1[r - 1, s] = p1s[r - 1, s]

    def scatter_done(r):
        wait_bytes(p1.at[r - 1, pl.ds(0, ns - 1)], p1_sem.at[r - 1])
        wait_bytes(p1.at[r - 1, pl.ds(0, ns - 1)], p1s_sem.at[r - 1])
        total = p1[r - 1, 0]
        for q in range(1, ns):
            total = total + p1[r - 1, q]
        return total

    resid = y_ref[...] - sum_blocks(0, block_rows)
    resid_b = share_resid(0, resid)

    diag = lax.broadcasted_iota(jnp.int32, (targets, targets), 0) == lax.broadcasted_iota(
        jnp.int32, (targets, targets), 1)
    ridge = jnp.sum(jnp.where(diag, jnp.broadcast_to(lam_ref[...], (targets, targets)), 0.0), axis=1, keepdims=True)
    eta_copy.wait()

    def sweep_chunk(c, resid_b):
        xc = xs[c]
        grad = jnp.dot(resid_b, xc, preferred_element_type=jnp.float32) / total_rows
        w = ws[c]
        step = eta[:, pl.ds(pl.multiple_of(c * cc, cc), cc)] * (grad - ridge * w)
        ws[c] = w + STEP_WEIGHT * step
        acc[...] += lax.dot_general(step.astype(jnp.bfloat16), xc, contract_last, preferred_element_type=jnp.float32)

    acc[...] = jnp.zeros_like(acc)
    forward(0)

    def sweep_first(c, carry):
        @pl.when(c + AHEAD + 1 < nch)
        def _():
            issue_first(c + AHEAD + 1)

        @pl.when(c + AHEAD < nch)
        def _():
            issue_direct(c + AHEAD)

        @pl.when(c + 1 < nch)
        def _():
            forward(c + 1)

        wait_bytes(xs.at[c], x_sem.at[c])
        wait_bytes(ws.at[c], w_sem.at[c])
        sweep_chunk(c, resid_b)
        return carry

    lax.fori_loop(0, nch, sweep_first, 0)

    def close_sweep(r, resid):
        scatter_start(r)
        return resid - STEP_WEIGHT * sum_blocks(r, scatter_done(r))

    for r in range(1, SWEEPS - 1):
        resid = close_sweep(r, resid)
        resid_b = share_resid(r, resid)
        acc[...] = jnp.zeros_like(acc)

        def sweep_middle(c, carry):
            sweep_chunk(c, resid_b)
            return carry

        lax.fori_loop(0, nch, sweep_middle, 0)

    resid = close_sweep(SWEEPS - 1, resid)
    resid_b = share_resid(SWEEPS - 1, resid)
    acc[...] = jnp.zeros_like(acc)

    def gather_direct(c):
        dst = wout_hbm.at[:, cols(s, c)]
        for peer in (right, left):
            remote(ws.at[c], dst, gs_sem.at[c], gd_sem.at[c], samp=peer).start()
        pltpu.make_async_copy(ws.at[c], dst, gs_sem.at[c]).start()

    def gather_forward(c):
        wait_bytes(wout_hbm.at[:, pl.ds(0, 2 * cc)], gd_sem.at[c])
        upper, lower = pl.ds(0, thalf), pl.ds(thalf, thalf)
        remote(wout_hbm.at[upper, cols(left, c)], wout_hbm.at[upper, cols(left, c)],
               gs_sem.at[c], gf_sem.at[c], samp=right).start()
        remote(wout_hbm.at[lower, cols(right, c)], wout_hbm.at[lower, cols(right, c)],
               gs_sem.at[c], gf_sem.at[c], samp=left).start()

    def sweep_last(c, carry):
        @pl.when((c > 0) & (c <= GATHER_FIRST))
        def _():
            gather_direct(c - 1)

        sweep_chunk(c, resid_b)
        return carry

    lax.fori_loop(0, nch, sweep_last, 0)
    scatter_start(SWEEPS)

    def gather_more(c, carry):
        gather_direct(c)
        return carry

    lax.fori_loop(GATHER_FIRST, GATHER_AHEAD, gather_more, 0)
    rout_ref[...] = resid - STEP_WEIGHT * sum_blocks(SWEEPS, scatter_done(SWEEPS))

    def gather_step(c, carry):
        gather_forward(c)

        @pl.when(c + GATHER_AHEAD < nch)
        def _():
            gather_direct(c + GATHER_AHEAD)

        return carry

    lax.fori_loop(0, nch, gather_step, 0)

    def drain(c, carry):
        wait_bytes(xs.at[c], xsend_sem.at[c])
        wait_bytes(wout_hbm.at[:, pl.ds(0, cc)], gf_sem.at[c])
        wait_bytes(wout_hbm.at[:, pl.ds(0, 4 * cc)], gs_sem.at[c])
        return carry

    lax.fori_loop(0, nch, drain, 0)


def solution(mesh):
    ns, nf = mesh.shape["samp"], mesh.shape["feat"]
    design_spec = P(("problem", "samp"), "feat")
    rows_spec = P(("problem", "samp"), None)
    coef_spec = P(("problem", "feat"), None)
    step_spec = P(("problem", "feat"))
    ridge_spec = P("problem")

    def local_sweeps(design, targets, coef_init, step_sizes, ridge_weights):
        rows, width = design.shape
        nt = targets.shape[1]
        quarter = width // ns
        nch = quarter // CHUNK
        dma = pltpu.SemaphoreType.DMA
        any_spec = pl.BlockSpec(memory_space=pl.ANY)
        vmem_spec = pl.BlockSpec(memory_space=pltpu.VMEM)
        coef_t, resid_t = pl.pallas_call(
            functools.partial(sweeps_kernel, ns, nf, rows * ns),
            out_shape=(jax.ShapeDtypeStruct((nt, width), jnp.float32),
                       jax.ShapeDtypeStruct((nt, rows), jnp.float32)),
            in_specs=[any_spec, vmem_spec, any_spec, any_spec, vmem_spec],
            out_specs=(any_spec, vmem_spec),
            scratch_shapes=[
                pltpu.VMEM((nch, rows * ns, CHUNK), jnp.bfloat16),
                pltpu.VMEM((nch, 2, rows // 2, CHUNK), jnp.bfloat16),
                pltpu.VMEM((nch, nt, CHUNK), jnp.float32),
                pltpu.VMEM((1, quarter), jnp.float32),
                pltpu.VMEM((nt, rows * ns), jnp.float32),
                pltpu.VMEM((STREAM_BUFS, rows, STREAM), jnp.bfloat16),
                pltpu.VMEM((STREAM_BUFS, nt, STREAM), jnp.float32),
                pltpu.VMEM((SWEEPS, ns, nt, rows), jnp.float32),
                pltpu.VMEM((SWEEPS, ns, nt, rows), jnp.float32),
                pltpu.VMEM((SWEEPS + 1, nf, nt, rows), jnp.bfloat16),
                pltpu.VMEM((SWEEPS, ns, nt, rows), jnp.bfloat16),
                dma((nch,)), dma((nch,)), dma((nch,)), dma((nch,)), dma, dma((STREAM_BUFS,)), dma((STREAM_BUFS,)),
                dma((SWEEPS,)), dma((SWEEPS,)), dma((SWEEPS + 1,)), dma((SWEEPS + 1,)), dma((SWEEPS,)), dma((SWEEPS,)),
                dma((nch,)), dma((nch,)), dma((nch,)),
            ],
            compiler_params=pltpu.CompilerParams(
                collective_id=0, has_side_effects=True, vmem_limit_bytes=66 * 1024 * 1024 - 2 * 1024 * 1024 - 65536),
            name="sweeps",
        )(design, targets.T, coef_init.T, step_sizes[None, :], ridge_weights[None, :])
        return coef_t.T, resid_t.T

    return jax.shard_map(
        local_sweeps, mesh=mesh, in_specs=(design_spec, rows_spec, coef_spec, step_spec, ridge_spec),
        out_specs=(coef_spec, rows_spec), check_vma=False)
```

time: 1520 us -> 598 us (0.39)
  waiting for transfers between devices: 1140 us -> 0 us
  Pallas kernels: 0 us -> 585 us
  matrix products: 201 us -> 0 us
  blocking collectives: 115 us -> 0 us
  other arithmetic: 48.3 us -> 0 us
    psum x4 -> x0, waiting for transfers between devices: 1140 us -> none  [local_sweeps(): gradient = lax.psum(part_grad, 'samp') / total_rows]
    pallas_call x0 -> x1, Pallas kernels: none -> 585 us  [local_sweeps(): pl.pallas_call(functools.partial(sweeps_kernel, ns, nf, rows * ns), out_s...]
    dot_general x9 -> x0, matrix products: 201 us -> none  [the longest x5 124 us: block_product(): jnp.dot(design, weights.astype(jnp.bfloat16), preferred_element_type=jnp....]
    psum x5 -> x0, blocking collectives: 115 us -> none  [the longest x4 90.9 us: local_sweeps(): lax.psum(block_product(step_delta), 'feat')]
    add x2 -> x0, other arithmetic: 47.7 us -> none  [local_sweeps(): coef_cur = coef_cur + STEP_WEIGHT * step_delta]
  transfers between devices with their start and end apart: 4 -> 0, of which waited for: 4 -> 0; matrix products, arithmetic and copies ran while one was open for 2% -> 0% of each run, Pallas kernels for 0% -> 0%
where the time goes in v1:
time: 598 us
  Pallas kernels  585 us (98%)
  local copies, waits for them, and re-layouts  12 us (2%)
    pallas_call x1, Pallas kernels, local_sweeps(): pl.pallas_call(functools.partial(sweeps_kernel, ns, nf, rows * ns), out_s...  585 us
    unnamed x4, local copies, waits for them, and re-layouts  12 us

profile of v1, /device:TPU:97, one launch (start us, length us, event | category | flops | bytes accessed | tf_op | source)
XLA Modules:
  0.0 597.8 jit_solution(11130414738976749475)
XLA Ops:
  0.6 585.1 %sweeps.1 = (f32[32,131072]{1,0:T(8,128)}, f32[32,128]{1,0:T(8,128)}) custom-call(bf16[128,131072]{1,0:T(8,128)(2,1)} %x_hbm.1, f32[32,128]{1,0:T(8,128)} %bitcast.9, f32[32,131072]{1,0:T(8,128)} %bitcast.6, f32[1,131072]{1,0:T(1,128)} %bitcast.8, f32[1,32]{1,0:T(1,128)} %bitcast.11), custom_call_target="tpu_custom_call" | custom-call | tf_op jit(solution)/shard_map/sweeps/pallas_call | solution.py:279
  585.8 0.0 copy-start
  585.8 11.4 %copy.9 = f32[131072,32]{0,1:T(8,128)} copy(f32[131072,32]{0,1:T(8,128)} %bitcast.7) | data formatting | bytes 33554432
  597.2 0.0 copy-done
  597.2 0.6 copy.10
Async XLA Ops:
  585.8 11.4 %copy-start = (f32[32,128]{1,0:T(8,128)S(1)}, f32[32,128]{1,0:T(8,128)}, u32[]{:S(2)}) copy-start(f32[32,128]{1,0:T(8,128)} %get-tuple-element.5) | copy-start | bytes 49156

commit v2 on v1

--- a/solution.py
+++ b/solution.py
@@ -9,27 +9,26 @@
 
 SWEEPS = 4
 STEP_WEIGHT = 0.5
-CHUNK = 1024
-AHEAD = 6
+CHUNK = 2048
+AHEAD = 4
 STREAM = 4096
-STREAM_BUFS = 4
-GATHER_FIRST = 8
-GATHER_AHEAD = 16
+STREAM_BUFS = 3
+GATHER_FIRST = 4
+GATHER_AHEAD = 8
 MESH = pl.DeviceIdType.MESH
 
 
 def sweeps_kernel(
     ns, nf, total_rows,
     x_hbm, y_ref, w0_hbm, eta_hbm, lam_ref,
-    wout_hbm, rout_ref,
-    xs, relay, ws, eta, acc, sx, sw, p1s, p1, p2, rb,
-    x_sem, xsend_sem, relay_sem, w_sem, eta_sem, sx_sem, sw_sem,
+    wout, rout_ref,
+    xs, eta, acc, sx, sw, p1s, p1, p2, rb,
+    x_sem, xsend_sem, w_sem, eta_sem, sx_sem, sw_sem,
     p1_sem, p1s_sem, p2_sem, p2s_sem, p3_sem, p3s_sem,
     gd_sem, gf_sem, gs_sem,
 ):
     nch, rows_all, cc = xs.shape
     rows = rows_all // ns
-    half = rows // 2
     targets = y_ref.shape[0]
     thalf = targets // 2
     quarter = nch * cc
@@ -58,25 +57,12 @@
         pl.semaphore_signal(barrier, inc=1, device_id={"feat": peer}, device_id_type=MESH)
     pl.semaphore_wait(barrier, ns - 1 + nf - 1)
 
-    def issue_first(c):
-        for part, peer in ((0, right), (1, left)):
-            remote(x_hbm.at[pl.ds(part * half, half), cols(opp, c)], relay.at[c, part],
-                   xsend_sem.at[c], relay_sem.at[c], samp=peer).start()
-
-    def issue_direct(c):
+    def issue(c):
         mine = pl.ds(pl.multiple_of(s * rows, rows), rows)
-        for peer in (right, left):
-            remote(x_hbm.at[:, cols(peer, c)], xs.at[c, mine, :],
-                   xsend_sem.at[c], x_sem.at[c], samp=peer).start()
+        for peer in (opp, right, left):
+            remote(x_hbm.at[:, cols(peer, c)], xs.at[c, mine, :], xsend_sem.at[c], x_sem.at[c], samp=peer).start()
         pltpu.make_async_copy(x_hbm.at[:, cols(s, c)], xs.at[c, mine, :], x_sem.at[c]).start()
-        pltpu.make_async_copy(w0_hbm.at[:, cols(s, c)], ws.at[c], w_sem.at[c]).start()
-
-    def forward(c):
-        wait_bytes(relay.at[c], relay_sem.at[c])
-        remote(relay.at[c, 0], xs.at[c, pl.ds(pl.multiple_of(left * rows, rows), half), :],
-               xsend_sem.at[c], x_sem.at[c], samp=right).start()
-        remote(relay.at[c, 1], xs.at[c, pl.ds(pl.multiple_of(right * rows + half, half), half), :],
-               xsend_sem.at[c], x_sem.at[c], samp=left).start()
+        pltpu.make_async_copy(w0_hbm.at[:, cols(s, c)], wout.at[:, cols(s, c)], w_sem.at[c]).start()
 
     def stream_copies(i):
         slot = lax.rem(i, STREAM_BUFS)
@@ -84,14 +70,12 @@
         return (pltpu.make_async_copy(x_hbm.at[:, span], sx.at[slot], sx_sem.at[slot]),
                 pltpu.make_async_copy(w0_hbm.at[:, span], sw.at[slot], sw_sem.at[slot]))
 
-    issue_first(0)
     for i in range(STREAM_BUFS - 1):
         for copy in stream_copies(i):
             copy.start()
 
     def issue_step(c, carry):
-        issue_first(c + 1)
-        issue_direct(c)
+        issue(c)
         return carry
 
     lax.fori_loop(0, AHEAD, issue_step, 0)
@@ -121,7 +105,6 @@
         for copy in copies:
             copy.start()
         wait_bytes(p2.at[r, pl.ds(0, nf - 1)], p2_sem.at[r])
-        wait_bytes(p2.at[r, pl.ds(0, nf - 1)], p2s_sem.at[r])
         total = p2[r, 0].astype(jnp.float32)
         for j in range(1, nf):
             total = total + p2[r, j].astype(jnp.float32)
@@ -132,7 +115,6 @@
         for peer in samp_peers:
             remote(rb.at[r, s], rb.at[r, s], p3s_sem.at[r], p3_sem.at[r], samp=peer).start()
         wait_bytes(rb.at[r, pl.ds(0, ns - 1)], p3_sem.at[r])
-        wait_bytes(rb.at[r, pl.ds(0, ns - 1)], p3s_sem.at[r])
         return jnp.concatenate([rb[r, q] for q in range(ns)], axis=1)
 
     def scatter_start(r):
@@ -144,7 +126,6 @@
 
     def scatter_done(r):
         wait_bytes(p1.at[r - 1, pl.ds(0, ns - 1)], p1_sem.at[r - 1])
-        wait_bytes(p1.at[r - 1, pl.ds(0, ns - 1)], p1s_sem.at[r - 1])
         total = p1[r - 1, 0]
         for q in range(1, ns):
             total = total + p1[r - 1, q]
@@ -161,29 +142,20 @@
     def sweep_chunk(c, resid_b):
         xc = xs[c]
         grad = jnp.dot(resid_b, xc, preferred_element_type=jnp.float32) / total_rows
-        w = ws[c]
+        w = wout[:, cols(s, c)]
         step = eta[:, pl.ds(pl.multiple_of(c * cc, cc), cc)] * (grad - ridge * w)
-        ws[c] = w + STEP_WEIGHT * step
+        wout[:, cols(s, c)] = w + STEP_WEIGHT * step
         acc[...] += lax.dot_general(step.astype(jnp.bfloat16), xc, contract_last, preferred_element_type=jnp.float32)
 
     acc[...] = jnp.zeros_like(acc)
-    forward(0)
 
     def sweep_first(c, carry):
-        @pl.when(c + AHEAD + 1 < nch)
-        def _():
-            issue_first(c + AHEAD + 1)
-
         @pl.when(c + AHEAD < nch)
         def _():
-            issue_direct(c + AHEAD)
-
-        @pl.when(c + 1 < nch)
-        def _():
-            forward(c + 1)
+            issue(c + AHEAD)
 
         wait_bytes(xs.at[c], x_sem.at[c])
-        wait_bytes(ws.at[c], w_sem.at[c])
+        wait_bytes(wout.at[:, pl.ds(0, cc)], w_sem.at[c])
         sweep_chunk(c, resid_b)
         return carry
 
@@ -209,18 +181,15 @@
     acc[...] = jnp.zeros_like(acc)
 
     def gather_direct(c):
-        dst = wout_hbm.at[:, cols(s, c)]
+        mine = wout.at[:, cols(s, c)]
         for peer in (right, left):
-            remote(ws.at[c], dst, gs_sem.at[c], gd_sem.at[c], samp=peer).start()
-        pltpu.make_async_copy(ws.at[c], dst, gs_sem.at[c]).start()
+            remote(mine, mine, gs_sem.at[c], gd_sem.at[c], samp=peer).start()
 
     def gather_forward(c):
-        wait_bytes(wout_hbm.at[:, pl.ds(0, 2 * cc)], gd_sem.at[c])
-        upper, lower = pl.ds(0, thalf), pl.ds(thalf, thalf)
-        remote(wout_hbm.at[upper, cols(left, c)], wout_hbm.at[upper, cols(left, c)],
-               gs_sem.at[c], gf_sem.at[c], samp=right).start()
-        remote(wout_hbm.at[lower, cols(right, c)], wout_hbm.at[lower, cols(right, c)],
-               gs_sem.at[c], gf_sem.at[c], samp=left).start()
+        wait_bytes(wout.at[:, pl.ds(0, 2 * cc)], gd_sem.at[c])
+        for part, peer, origin in ((0, right, left), (1, left, right)):
+            theirs = wout.at[pl.ds(part * thalf, thalf), cols(origin, c)]
+            remote(theirs, theirs, gs_sem.at[c], gf_sem.at[c], samp=peer).start()
 
     def sweep_last(c, carry):
         @pl.when((c > 0) & (c <= GATHER_FIRST))
@@ -252,12 +221,17 @@
     lax.fori_loop(0, nch, gather_step, 0)
 
     def drain(c, carry):
-        wait_bytes(xs.at[c], xsend_sem.at[c])
-        wait_bytes(wout_hbm.at[:, pl.ds(0, cc)], gf_sem.at[c])
-        wait_bytes(wout_hbm.at[:, pl.ds(0, 4 * cc)], gs_sem.at[c])
+        wait_bytes(xs.at[c, pl.ds(0, rows_all - rows)], xsend_sem.at[c])
+        wait_bytes(wout.at[:, pl.ds(0, cc)], gf_sem.at[c])
+        wait_bytes(wout.at[:, pl.ds(0, 3 * cc)], gs_sem.at[c])
         return carry
 
     lax.fori_loop(0, nch, drain, 0)
+    for r in range(SWEEPS + 1):
+        wait_bytes(p2.at[r, pl.ds(0, nf - 1)], p2s_sem.at[r])
+    for r in range(SWEEPS):
+        wait_bytes(rb.at[r, pl.ds(0, ns - 1)], p3s_sem.at[r])
+        wait_bytes(p1.at[r, pl.ds(0, ns - 1)], p1s_sem.at[r])
 
 
 def solution(mesh):
@@ -278,14 +252,12 @@
         vmem_spec = pl.BlockSpec(memory_space=pltpu.VMEM)
         coef_t, resid_t = pl.pallas_call(
             functools.partial(sweeps_kernel, ns, nf, rows * ns),
-            out_shape=(jax.ShapeDtypeStruct((nt, width), jnp.float32),
+            out_shape=(pltpu.VMEM((nt, width), jnp.float32),
                        jax.ShapeDtypeStruct((nt, rows), jnp.float32)),
             in_specs=[any_spec, vmem_spec, any_spec, any_spec, vmem_spec],
-            out_specs=(any_spec, vmem_spec),
+            out_specs=(vmem_spec, vmem_spec),
             scratch_shapes=[
                 pltpu.VMEM((nch, rows * ns, CHUNK), jnp.bfloat16),
-                pltpu.VMEM((nch, 2, rows // 2, CHUNK), jnp.bfloat16),
-                pltpu.VMEM((nch, nt, CHUNK), jnp.float32),
                 pltpu.VMEM((1, quarter), jnp.float32),
                 pltpu.VMEM((nt, rows * ns), jnp.float32),
                 pltpu.VMEM((STREAM_BUFS, rows, STREAM), jnp.bfloat16),
@@ -294,12 +266,12 @@
                 pltpu.VMEM((SWEEPS, ns, nt, rows), jnp.float32),
                 pltpu.VMEM((SWEEPS + 1, nf, nt, rows), jnp.bfloat16),
                 pltpu.VMEM((SWEEPS, ns, nt, rows), jnp.bfloat16),
-                dma((nch,)), dma((nch,)), dma((nch,)), dma((nch,)), dma, dma((STREAM_BUFS,)), dma((STREAM_BUFS,)),
+                dma((nch,)), dma((nch,)), dma((nch,)), dma, dma((STREAM_BUFS,)), dma((STREAM_BUFS,)),
                 dma((SWEEPS,)), dma((SWEEPS,)), dma((SWEEPS + 1,)), dma((SWEEPS + 1,)), dma((SWEEPS,)), dma((SWEEPS,)),
                 dma((nch,)), dma((nch,)), dma((nch,)),
             ],
             compiler_params=pltpu.CompilerParams(
-                collective_id=0, has_side_effects=True, vmem_limit_bytes=66 * 1024 * 1024 - 2 * 1024 * 1024 - 65536),
+                collective_id=0, has_side_effects=True, vmem_limit_bytes=47 * 1024 * 1024),
             name="sweeps",
         )(design, targets.T, coef_init.T, step_sizes[None, :], ridge_weights[None, :])
         return coef_t.T, resid_t.T

time: 598 us -> 587 us (0.982)
  Pallas kernels: 585 us -> 579 us
    pallas_call x1, Pallas kernels: 585 us -> 579 us  [local_sweeps(): pl.pallas_call(functools.partial(sweeps_kernel, ns, nf, rows * ns), out_s...]
where the time goes in v2:
time: 587 us
  Pallas kernels  579 us (99%)
  local copies, waits for them, and re-layouts  6.77 us (1%)
    pallas_call x1, Pallas kernels, local_sweeps(): pl.pallas_call(functools.partial(sweeps_kernel, ns, nf, rows * ns), out_s...  579 us

profile of v2, /device:TPU:97, one launch (start us, length us, event | category | flops | bytes accessed | tf_op | source)
XLA Modules:
  0.0 586.5 jit_solution(4806700166660509212)
XLA Ops:
  0.6 579.1 %sweeps.1 = (f32[32,131072]{1,0:T(8,128)S(1)}, f32[32,128]{1,0:T(8,128)}) custom-call(bf16[128,131072]{1,0:T(8,128)(2,1)} %x_hbm.1, f32[32,128]{1,0:T(8,128)} %bitcast.9, f32[32,131072]{1,0:T(8,128)} %bitcast.7, f32[1,131072]{1,0:T(1,128)} %bitcast.8, f32[1,32]{1,0:T(1,128)} %bitcast.11), custom_call_target="tpu_custom_call" | custom-call | tf_op jit(solution)/shard_map/sweeps/pallas_call | solution.py:253
  579.8 0.0 copy-start
  579.8 6.2 %copy.9 = f32[131072,32]{0,1:T(8,128)} copy(f32[131072,32]{0,1:T(8,128)S(1)} %bitcast.6) | data formatting | bytes 33554432
  585.9 0.0 copy-done
  585.9 0.6 copy.10
Async XLA Ops:
  579.8 6.2 %copy-start = (f32[32,128]{1,0:T(8,128)S(1)}, f32[32,128]{1,0:T(8,128)}, u32[]{:S(2)}) copy-start(f32[32,128]{1,0:T(8,128)} %get-tuple-element.5) | copy-start | bytes 49156

commit v3 on v2

--- a/solution.py
+++ b/solution.py
@@ -15,6 +15,7 @@
 STREAM_BUFS = 3
 GATHER_FIRST = 4
 GATHER_AHEAD = 8
+UNROLL = 4
 MESH = pl.DeviceIdType.MESH
 
 
@@ -22,9 +23,9 @@
     ns, nf, total_rows,
     x_hbm, y_ref, w0_hbm, eta_hbm, lam_ref,
     wout, rout_ref,
-    xs, eta, acc, sx, sw, p1s, p1, p2, rb,
+    xs, eta, acc, sx, sw, p1s, p1, p2, pm, rs,
     x_sem, xsend_sem, w_sem, eta_sem, sx_sem, sw_sem,
-    p1_sem, p1s_sem, p2_sem, p2s_sem, p3_sem, p3s_sem,
+    p1_sem, p1s_sem, p2_sem, p2s_sem, pm_sem, pms_sem, rs_sem, rss_sem,
     gd_sem, gf_sem, gs_sem,
 ):
     nch, rows_all, cc = xs.shape
@@ -36,8 +37,11 @@
     s = lax.axis_index("samp")
     f = lax.axis_index("feat")
     right, left, opp = lax.rem(s + 1, ns), lax.rem(s + ns - 1, ns), lax.rem(s + 2, ns)
-    samp_peers = [lax.rem(s + k, ns) for k in range(1, ns)]
+    samp_peers = [opp, right, left]
     feat_peers = [lax.rem(f + k, nf) for k in range(1, nf)]
+    far_first = sorted(((i, j) for i in range(ns) for j in range(nf) if i or j),
+                       key=lambda d: -min(d[0], ns - d[0]) - min(d[1], nf - d[1]) / 2)
+    group = [{"samp": lax.rem(s + i, ns), "feat": lax.rem(f + j, nf)} for i, j in far_first]
 
     def remote(src, dst, send_sem, recv_sem, **where):
         return pltpu.make_async_remote_copy(
@@ -51,11 +55,9 @@
         pltpu.make_async_copy(ref, ref, sem).wait()
 
     barrier = pltpu.get_barrier_semaphore()
-    for peer in samp_peers:
-        pl.semaphore_signal(barrier, inc=1, device_id={"samp": peer}, device_id_type=MESH)
-    for peer in feat_peers:
-        pl.semaphore_signal(barrier, inc=1, device_id={"feat": peer}, device_id_type=MESH)
-    pl.semaphore_wait(barrier, ns - 1 + nf - 1)
+    for peer in group:
+        pl.semaphore_signal(barrier, inc=1, device_id=peer, device_id_type=MESH)
+    pl.semaphore_wait(barrier, len(group))
 
     def issue(c):
         mine = pl.ds(pl.multiple_of(s * rows, rows), rows)
@@ -110,12 +112,20 @@
             total = total + p2[r, j].astype(jnp.float32)
         return total
 
-    def share_resid(r, resid):
-        rb[r, s] = resid.astype(jnp.bfloat16)
-        for peer in samp_peers:
-            remote(rb.at[r, s], rb.at[r, s], p3s_sem.at[r], p3_sem.at[r], samp=peer).start()
-        wait_bytes(rb.at[r, pl.ds(0, ns - 1)], p3_sem.at[r])
-        return jnp.concatenate([rb[r, q] for q in range(ns)], axis=1)
+    def sum_blocks_all(r, block_rows):
+        pm[r - 1, s * nf + f] = block_rows.astype(jnp.bfloat16)
+        mine = pm.at[r - 1, s * nf + f]
+        for peer in group:
+            remote(mine, mine, pms_sem.at[r - 1], pm_sem.at[r - 1], **peer).start()
+        wait_bytes(pm.at[r - 1, pl.ds(0, ns * nf - 1)], pm_sem.at[r - 1])
+        for q in range(ns):
+            total = pm[r - 1, q * nf].astype(jnp.float32)
+            for j in range(1, nf):
+                total = total + pm[r - 1, q * nf + j].astype(jnp.float32)
+            rs[q] = rs[q] - STEP_WEIGHT * total
+
+    def rounded_resid():
+        return jnp.concatenate([rs[q].astype(jnp.bfloat16) for q in range(ns)], axis=1)
 
     def scatter_start(r):
         for q in range(ns):
@@ -131,8 +141,12 @@
             total = total + p1[r - 1, q]
         return total
 
-    resid = y_ref[...] - sum_blocks(0, block_rows)
-    resid_b = share_resid(0, resid)
+    rs[s] = y_ref[...] - sum_blocks(0, block_rows)
+    for peer in samp_peers:
+        remote(rs.at[s], rs.at[s], rss_sem, rs_sem, samp=peer).start()
+    wait_bytes(rs.at[pl.ds(0, ns - 1)], rs_sem)
+    wait_bytes(rs.at[pl.ds(0, ns - 1)], rss_sem)
+    resid_b = rounded_resid()
 
     diag = lax.broadcasted_iota(jnp.int32, (targets, targets), 0) == lax.broadcasted_iota(
         jnp.int32, (targets, targets), 1)
@@ -161,24 +175,22 @@
 
     lax.fori_loop(0, nch, sweep_first, 0)
 
-    def close_sweep(r, resid):
+    def close_sweep(r):
         scatter_start(r)
-        return resid - STEP_WEIGHT * sum_blocks(r, scatter_done(r))
+        sum_blocks_all(r, scatter_done(r))
+        acc[...] = jnp.zeros_like(acc)
+        return rounded_resid()
 
     for r in range(1, SWEEPS - 1):
-        resid = close_sweep(r, resid)
-        resid_b = share_resid(r, resid)
-        acc[...] = jnp.zeros_like(acc)
+        resid_b = close_sweep(r)
 
         def sweep_middle(c, carry):
             sweep_chunk(c, resid_b)
             return carry
 
-        lax.fori_loop(0, nch, sweep_middle, 0)
-
-    resid = close_sweep(SWEEPS - 1, resid)
-    resid_b = share_resid(SWEEPS - 1, resid)
-    acc[...] = jnp.zeros_like(acc)
+        lax.fori_loop(0, nch, sweep_middle, 0, unroll=UNROLL)
+
+    resid_b = close_sweep(SWEEPS - 1)
 
     def gather_direct(c):
         mine = wout.at[:, cols(s, c)]
@@ -207,7 +219,7 @@
         return carry
 
     lax.fori_loop(GATHER_FIRST, GATHER_AHEAD, gather_more, 0)
-    rout_ref[...] = resid - STEP_WEIGHT * sum_blocks(SWEEPS, scatter_done(SWEEPS))
+    rout_ref[...] = rs[s] - STEP_WEIGHT * sum_blocks(1, scatter_done(SWEEPS))
 
     def gather_step(c, carry):
         gather_forward(c)
@@ -227,10 +239,11 @@
         return carry
 
     lax.fori_loop(0, nch, drain, 0)
-    for r in range(SWEEPS + 1):
+    for r in range(2):
         wait_bytes(p2.at[r, pl.ds(0, nf - 1)], p2s_sem.at[r])
+    for r in range(SWEEPS - 1):
+        wait_bytes(pm.at[r, pl.ds(0, ns * nf - 1)], pms_sem.at[r])
     for r in range(SWEEPS):
-        wait_bytes(rb.at[r, pl.ds(0, ns - 1)], p3s_sem.at[r])
         wait_bytes(p1.at[r, pl.ds(0, ns - 1)], p1s_sem.at[r])
 
 
@@ -264,10 +277,11 @@
                 pltpu.VMEM((STREAM_BUFS, nt, STREAM), jnp.float32),
                 pltpu.VMEM((SWEEPS, ns, nt, rows), jnp.float32),
                 pltpu.VMEM((SWEEPS, ns, nt, rows), jnp.float32),
-                pltpu.VMEM((SWEEPS + 1, nf, nt, rows), jnp.bfloat16),
-                pltpu.VMEM((SWEEPS, ns, nt, rows), jnp.bfloat16),
+                pltpu.VMEM((2, nf, nt, rows), jnp.bfloat16),
+                pltpu.VMEM((SWEEPS - 1, ns * nf, nt, rows), jnp.bfloat16),
+                pltpu.VMEM((ns, nt, rows), jnp.float32),
                 dma((nch,)), dma((nch,)), dma((nch,)), dma, dma((STREAM_BUFS,)), dma((STREAM_BUFS,)),
-                dma((SWEEPS,)), dma((SWEEPS,)), dma((SWEEPS + 1,)), dma((SWEEPS + 1,)), dma((SWEEPS,)), dma((SWEEPS,)),
+                dma((SWEEPS,)), dma((SWEEPS,)), dma((2,)), dma((2,)), dma((SWEEPS - 1,)), dma((SWEEPS - 1,)), dma, dma,
                 dma((nch,)), dma((nch,)), dma((nch,)),
             ],
             compiler_params=pltpu.CompilerParams(

time: 587 us -> 581 us (0.990)
  no operation moved by 1% of the time
where the time goes in v3:
time: 581 us
  Pallas kernels  574 us (99%)
  local copies, waits for them, and re-layouts  6.77 us (1%)
    pallas_call x1, Pallas kernels, local_sweeps(): pl.pallas_call(functools.partial(sweeps_kernel, ns, nf, rows * ns), out_s...  574 us

profile of v3, /device:TPU:97, one launch (start us, length us, event | category | flops | bytes accessed | tf_op | source)
XLA Modules:
  0.0 581.1 jit_solution(11609388737560560536)
XLA Ops:
  0.6 573.7 %sweeps.1 = (f32[32,131072]{1,0:T(8,128)S(1)}, f32[32,128]{1,0:T(8,128)}) custom-call(bf16[128,131072]{1,0:T(8,128)(2,1)} %x_hbm.1, f32[32,128]{1,0:T(8,128)} %bitcast.9, f32[32,131072]{1,0:T(8,128)} %bitcast.7, f32[1,131072]{1,0:T(1,128)} %bitcast.8, f32[1,32]{1,0:T(1,128)} %bitcast.11), custom_call_target="tpu_custom_call" | custom-call | tf_op jit(solution)/shard_map/sweeps/pallas_call | solution.py:266
  574.4 0.0 copy-start
  574.4 6.2 %copy.9 = f32[131072,32]{0,1:T(8,128)} copy(f32[131072,32]{0,1:T(8,128)S(1)} %bitcast.6) | data formatting | bytes 33554432
  580.5 0.0 copy-done
  580.5 0.6 copy.10
Async XLA Ops:
  574.4 6.2 %copy-start = (f32[32,128]{1,0:T(8,128)S(1)}, f32[32,128]{1,0:T(8,128)}, u32[]{:S(2)}) copy-start(f32[32,128]{1,0:T(8,128)} %get-tuple-element.5) | copy-start | bytes 49156

commit v4 on v3

--- a/solution.py
+++ b/solution.py
@@ -15,7 +15,7 @@
 STREAM_BUFS = 3
 GATHER_FIRST = 4
 GATHER_AHEAD = 8
-UNROLL = 4
+UNROLL = 8
 MESH = pl.DeviceIdType.MESH
 
 
@@ -23,7 +23,7 @@
     ns, nf, total_rows,
     x_hbm, y_ref, w0_hbm, eta_hbm, lam_ref,
     wout, rout_ref,
-    xs, eta, acc, sx, sw, p1s, p1, p2, pm, rs,
+    xs, sb, eta, acc, sx, sw, p1s, p1, p2, pm, rs,
     x_sem, xsend_sem, w_sem, eta_sem, sx_sem, sw_sem,
     p1_sem, p1s_sem, p2_sem, p2s_sem, pm_sem, pms_sem, rs_sem, rss_sem,
     gd_sem, gf_sem, gs_sem,
@@ -175,22 +175,40 @@
 
     lax.fori_loop(0, nch, sweep_first, 0)
 
-    def close_sweep(r):
-        scatter_start(r)
+    def middle_sweep(r, resid_b):
+        def step_chunk(c, carry):
+            grad = jnp.dot(resid_b, xs[c], preferred_element_type=jnp.float32) / total_rows
+            w = wout[:, cols(s, c)]
+            step = eta[:, pl.ds(pl.multiple_of(c * cc, cc), cc)] * (grad - ridge * w)
+            wout[:, cols(s, c)] = w + STEP_WEIGHT * step
+            sb[c] = step.astype(jnp.bfloat16)
+            return carry
+
+        lax.fori_loop(0, nch, step_chunk, 0, unroll=UNROLL)
+
+        def block_product(q):
+            block = pl.ds(pl.multiple_of(q * rows, rows), rows)
+            total = jnp.zeros((rows, targets), jnp.float32)
+            for c in range(nch):
+                total = total + lax.dot_general(xs[c, block, :], sb[c], contract_last, preferred_element_type=jnp.float32)
+            return total.T
+
+        def peer_block(p, carry):
+            q = lax.rem(s + 1 + p, ns)
+            p1s[r - 1, q] = block_product(q)
+            remote(p1s.at[r - 1, q], p1.at[r - 1, s], p1s_sem.at[r - 1], p1_sem.at[r - 1], samp=q).start()
+            return carry
+
+        lax.fori_loop(0, ns - 1, peer_block, 0)
+        p1[r - 1, s] = block_product(s)
+
+    scatter_start(1)
+    sum_blocks_all(1, scatter_done(1))
+    for r in range(2, SWEEPS):
+        middle_sweep(r, rounded_resid())
         sum_blocks_all(r, scatter_done(r))
-        acc[...] = jnp.zeros_like(acc)
-        return rounded_resid()
-
-    for r in range(1, SWEEPS - 1):
-        resid_b = close_sweep(r)
-
-        def sweep_middle(c, carry):
-            sweep_chunk(c, resid_b)
-            return carry
-
-        lax.fori_loop(0, nch, sweep_middle, 0, unroll=UNROLL)
-
-    resid_b = close_sweep(SWEEPS - 1)
+    resid_b = rounded_resid()
+    acc[...] = jnp.zeros_like(acc)
 
     def gather_direct(c):
         mine = wout.at[:, cols(s, c)]
@@ -271,6 +289,7 @@
             out_specs=(vmem_spec, vmem_spec),
             scratch_shapes=[
                 pltpu.VMEM((nch, rows * ns, CHUNK), jnp.bfloat16),
+                pltpu.VMEM((nch, nt, CHUNK), jnp.bfloat16),
                 pltpu.VMEM((1, quarter), jnp.float32),
                 pltpu.VMEM((nt, rows * ns), jnp.float32),
                 pltpu.VMEM((STREAM_BUFS, rows, STREAM), jnp.bfloat16),

time: 581 us -> 574 us (0.988)
  Pallas kernels: 574 us -> 566 us
    pallas_call x1, Pallas kernels: 574 us -> 566 us  [local_sweeps(): pl.pallas_call(functools.partial(sweeps_kernel, ns, nf, rows * ns), out_s...]
where the time goes in v4:
time: 574 us
  Pallas kernels  566 us (99%)
  local copies, waits for them, and re-layouts  6.77 us (1%)
    pallas_call x1, Pallas kernels, local_sweeps(): pl.pallas_call(functools.partial(sweeps_kernel, ns, nf, rows * ns), out_s...  566 us

profile of v4, /device:TPU:97, one launch (start us, length us, event | category | flops | bytes accessed | tf_op | source)
XLA Modules:
  0.0 573.8 jit_solution(3703699965930755464)
XLA Ops:
  0.6 566.4 %sweeps.1 = (f32[32,131072]{1,0:T(8,128)S(1)}, f32[32,128]{1,0:T(8,128)}) custom-call(bf16[128,131072]{1,0:T(8,128)(2,1)} %x_hbm.1, f32[32,128]{1,0:T(8,128)} %bitcast.9, f32[32,131072]{1,0:T(8,128)} %bitcast.7, f32[1,131072]{1,0:T(1,128)} %bitcast.8, f32[1,32]{1,0:T(1,128)} %bitcast.11), custom_call_target="tpu_custom_call" | custom-call | tf_op jit(solution)/shard_map/sweeps/pallas_call | solution.py:284
  567.0 0.0 copy-start
  567.1 6.2 %copy.9 = f32[131072,32]{0,1:T(8,128)} copy(f32[131072,32]{0,1:T(8,128)S(1)} %bitcast.6) | data formatting | bytes 33554432
  573.2 0.0 copy-done
  573.2 0.6 copy.10
Async XLA Ops:
  567.0 6.2 %copy-start = (f32[32,128]{1,0:T(8,128)S(1)}, f32[32,128]{1,0:T(8,128)}, u32[]{:S(2)}) copy-start(f32[32,128]{1,0:T(8,128)} %get-tuple-element.5) | copy-start | bytes 49156

commit v5 on v4

--- a/solution.py
+++ b/solution.py
@@ -175,8 +175,13 @@
 
     lax.fori_loop(0, nch, sweep_first, 0)
 
-    def middle_sweep(r, resid_b):
+    def later_sweep(r, resid_b):
         def step_chunk(c, carry):
+            if r == SWEEPS:
+                @pl.when((c > 0) & (c <= GATHER_FIRST))
+                def _():
+                    gather_direct(c - 1)
+
             grad = jnp.dot(resid_b, xs[c], preferred_element_type=jnp.float32) / total_rows
             w = wout[:, cols(s, c)]
             step = eta[:, pl.ds(pl.multiple_of(c * cc, cc), cc)] * (grad - ridge * w)
@@ -205,10 +210,8 @@
     scatter_start(1)
     sum_blocks_all(1, scatter_done(1))
     for r in range(2, SWEEPS):
-        middle_sweep(r, rounded_resid())
+        later_sweep(r, rounded_resid())
         sum_blocks_all(r, scatter_done(r))
-    resid_b = rounded_resid()
-    acc[...] = jnp.zeros_like(acc)
 
     def gather_direct(c):
         mine = wout.at[:, cols(s, c)]
@@ -221,16 +224,7 @@
             theirs = wout.at[pl.ds(part * thalf, thalf), cols(origin, c)]
             remote(theirs, theirs, gs_sem.at[c], gf_sem.at[c], samp=peer).start()
 
-    def sweep_last(c, carry):
-        @pl.when((c > 0) & (c <= GATHER_FIRST))
-        def _():
-            gather_direct(c - 1)
-
-        sweep_chunk(c, resid_b)
-        return carry
-
-    lax.fori_loop(0, nch, sweep_last, 0)
-    scatter_start(SWEEPS)
+    later_sweep(SWEEPS, rounded_resid())
 
     def gather_more(c, carry):
         gather_direct(c)

time: 574 us -> 573 us (level)
  no operation moved by 1% of the time
where the time goes in v5:
time: 573 us
  Pallas kernels  566 us (99%)
  local copies, waits for them, and re-layouts  6.77 us (1%)
    pallas_call x1, Pallas kernels, local_sweeps(): pl.pallas_call(functools.partial(sweeps_kernel, ns, nf, rows * ns), out_s...  566 us

profile of v5, /device:TPU:97, one launch (start us, length us, event | category | flops | bytes accessed | tf_op | source)
XLA Modules:
  0.0 573.2 jit_solution(7534353033790769584)
XLA Ops:
  0.6 565.8 %sweeps.1 = (f32[32,131072]{1,0:T(8,128)S(1)}, f32[32,128]{1,0:T(8,128)}) custom-call(bf16[128,131072]{1,0:T(8,128)(2,1)} %x_hbm.1, f32[32,128]{1,0:T(8,128)} %bitcast.9, f32[32,131072]{1,0:T(8,128)} %bitcast.7, f32[1,131072]{1,0:T(1,128)} %bitcast.8, f32[1,32]{1,0:T(1,128)} %bitcast.11), custom_call_target="tpu_custom_call" | custom-call | tf_op jit(solution)/shard_map/sweeps/pallas_call | solution.py:278
  566.4 0.0 copy-start
  566.4 6.2 %copy.9 = f32[131072,32]{0,1:T(8,128)} copy(f32[131072,32]{0,1:T(8,128)S(1)} %bitcast.6) | data formatting | bytes 33554432
  572.6 0.0 copy-done
  572.6 0.6 copy.10
Async XLA Ops:
  566.4 6.2 %copy-start = (f32[32,128]{1,0:T(8,128)S(1)}, f32[32,128]{1,0:T(8,128)}, u32[]{:S(2)}) copy-start(f32[32,128]{1,0:T(8,128)} %get-tuple-element.5) | copy-start | bytes 49156
